TPU v7x, 32 devices: a whole 2x2x4 slice. The times are simulated.
32 devices in a mesh: row: 4 (over y, core), col: 8 (over z, x).
Axes of the slice: x: 2, y: 2, z: 4, core: 2. Of those that a mesh axis runs over, the one named last changes fastest.
Arguments:
- vectors: bfloat16 [4, 8, 128, 384], P('row', 'col'), may hold values from -6 to 6
- near_blocks: bfloat16 [4, 8, 9, 384, 384], P('row', 'col'), may hold values from -0.15625 to 0.15625
- near_source: int32 [4, 8, 9], P('row', 'col'), may hold values from 0 to 8, each once within a row
- near_count: int32 [4, 8], P('row', 'col'), may hold values from 1 to 9
- basis_col: bfloat16 [4, 8, 64, 384], P('row', 'col'), may hold values from -0.3125 to 0.3125
- transfer_col: bfloat16 [4, 8, 64, 64], P('row', 'col'), may hold values from -0.25 to 0.25
- leaf_couple: bfloat16 [4, 8, 3, 5, 64, 64], P('row', 'col'), may hold values from -0.1875 to 0.1875
- coupling: bfloat16 [4, 4, 64, 64], P('row'), may hold values from -0.75 to 0.75
- distant_region_list: int32 [4, 4], P('row'), may hold values from 0 to 3, each once within a row
- transfer_row: bfloat16 [4, 8, 64, 64], P('row', 'col'), may hold values from -0.75 to 0.75
- basis_row: bfloat16 [4, 8, 64, 384], P('row', 'col'), may hold values from -0.75 to 0.75
Outputs:
- product: bfloat16 [4, 8, 128, 384], P('row', 'col')
Inputs may be any that keep to these rules, and one draw needn't show every extreme that they name: `near_source`: the 9 slots of a leaf name the nine neighbourhood cells once each. Only the first near_count slots of a leaf are live. `distant_region_list`: each region's list names every region once.
All inputs are finite; a program needn't handle non-finite values.
Results may differ from a plain program's by a relative error of at most 0.013.
Values may be sent and summed in bfloat16 or wider, within the bound.
A program may use at most 64 MiB of HBM per device.

v0:
```python
import jax
import jax.numpy as jnp
from jax import lax
from jax.sharding import PartitionSpec as P


def from_behind(value, axis, steps):
    count = lax.axis_size(axis)
    pairs = [(source, (source + steps) % count) for source in range(count)]
    return lax.ppermute(value, axis, pairs)


def padded_2(cells, sides, width):
    for axis, dim in sides:
        count = lax.axis_size(axis)
        head = lax.slice_in_dim(cells, 0, width, axis=dim)
        tail = lax.slice_in_dim(cells, cells.shape[dim] - width, cells.shape[dim], axis=dim)
        cells = jnp.concatenate(
            [
                lax.ppermute(tail, axis, [(i, (i + 1) % count) for i in range(count)]),
                cells,
                lax.ppermute(head, axis, [((i + 1) % count, i) for i in range(count)]),
            ],
            axis=dim,
        )
    return cells


def per_device(
    vectors,
    near_blocks,
    near_source,
    near_count,
    basis_col,
    transfer_col,
    leaf_couple,
    coupling,
    distant_region_list,
    transfer_row,
    basis_row,
):
    upper_limit = lax.Precision.HIGHEST
    leading = from_behind(vectors, "row", -1)
    leading = from_behind(leading, "col", -1)
    padded = padded_2(leading, (("row", 0), ("col", 1)), 1)
    table = padded.reshape(9, padded.shape[2], padded.shape[3])
    picked = jnp.take(table, near_source[0, 0], axis=0)
    slots = jnp.arange(picked.shape[0], dtype=jnp.int32)
    live_mask = (slots < near_count[0, 0])[:, None, None]
    picked = jnp.where(live_mask, picked, jnp.zeros_like(picked))
    near_part = jnp.einsum(
        "svp,spq->vq", picked, near_blocks[0, 0], preferred_element_type=jnp.float32
    )
    incoming_leaf = lax.dot_general(
        vectors[0, 0], basis_col[0, 0], (((1,), (1,)), ((), ())), preferred_element_type=jnp.float32
    )
    next_row = from_behind(incoming_leaf.astype(jnp.bfloat16), "row", -1).astype(
        incoming_leaf.dtype
    )
    second_row = from_behind(incoming_leaf.astype(jnp.bfloat16), "row", -2).astype(
        incoming_leaf.dtype
    )
    three_rows = jnp.stack([incoming_leaf, next_row, second_row], axis=0)
    leaves_of_rows = lax.all_gather(
        three_rows[:, None].astype(jnp.bfloat16), "col", axis=1, tiled=True
    ).astype(jnp.float32)
    col_count = lax.axis_size("col")
    rolled = jnp.roll(leaves_of_rows, -(lax.axis_index("col") + 3), axis=1)[:, : col_count - 3]
    band = jnp.einsum(
        "dfvk,dfkl->vl", rolled, leaf_couple[0, 0].astype(jnp.float32), precision=upper_limit
    )
    upward = jnp.dot(incoming_leaf, transfer_col[0, 0].astype(jnp.float32), precision=upper_limit)
    row_count = lax.axis_size("row")
    own_region = lax.psum(upward.astype(jnp.bfloat16), "col").astype(jnp.float32)
    regions = lax.all_gather(
        own_region[None].astype(jnp.bfloat16), "row", axis=0, tiled=True
    ).astype(jnp.float32)
    listing = distant_region_list[0]
    far_mask = ((listing - lax.axis_index("row")) % row_count >= 3).astype(jnp.float32)
    far_coeff = jnp.take(regions, listing, axis=0) * far_mask[:, None, None]
    outgoing_region = jnp.einsum(
        "fvk,fkl->vl", far_coeff, coupling[0].astype(jnp.float32), precision=upper_limit
    )
    leaf_out = band + jnp.dot(
        outgoing_region, transfer_row[0, 0].astype(jnp.float32), precision=upper_limit
    )
    far_part = jnp.dot(leaf_out, basis_row[0, 0].astype(jnp.float32), precision=upper_limit)
    return (near_part + far_part).astype(jnp.bfloat16)[None, None]


def solution(mesh):
    placed = (
        P("row", "col", None, None),
        P("row", "col", None, None, None),
        P("row", "col", None),
        P("row", "col"),
        P("row", "col", None, None),
        P("row", "col", None, None),
        P("row", "col", None, None, None, None),
        P("row", None, None, None),
        P("row", None),
        P("row", "col", None, None),
        P("row", "col", None, None),
    )
    return jax.shard_map(
        per_device,
        mesh=mesh,
        in_specs=placed,
        out_specs=P("row", "col", None, None),
        check_vma=False,
    )
```

profile of v0, /device:TPU:0, one launch (start us, length us, event | category | flops | bytes accessed | tf_op | source)
XLA Modules:
  0.0 111.8 jit_solution(17042163950172736035)
XLA Ops:
  0.0 0.0 copy-start
  0.0 0.0 copy-start.3
  0.0 2.4 %collective-permute-start = (bf16[1,1,128,384]{3,2,1,0:T(8,128)(2,1)}, bf16[1,1,128,384]{3,2,1,0:T(8,128)(2,1)S(1)}, u32[]{:S(2)}, u32[]{:S(2)}) collective-permute-start(bf16[1,1,128,384]{3,2,1,0:T(8,128)(2,1)} %param.11), channel_id=1, source_target_pairs={{0,24},{8,0},{16,8},{24,16},{1,25},{9,1},{17,9},{25,17},{2,26},{10... | collective-permute-start | bytes 294920 | tf_op jit(solution)/shard_map/ppermute | solution.py:10
  2.4 1.1 fusion.37
  3.5 0.8 collective-permute-start.7
  4.3 0.1 collective-permute-start.6
  4.4 0.7 fusion.30
  5.7 0.7 compare_and_fusion.1
  6.4 0.9 fusion.7
  7.3 37.6 %psum.7 = bf16[1,128,64]{1,2,0:T(8,128)(2,1)S(1)} all-reduce(bf16[1,128,64]{1,2,0:T(8,128)(2,1)S(1)} %fusion.7), channel_id=1, replica_groups=mesh['row'=4,'col'=8] {'col'}, use_global_device_ids=true, to_apply=%region_0.1 | all-reduce | flops 8192 | bytes 32768 | tf_op jit(solution)/shard_map/psum | solution.py:74
  44.9 5.2 %all_gather.7 = bf16[4,128,64]{1,2,0:T(8,128)(2,1)S(1)} all-gather(bf16[1,128,64]{1,2,0:T(8,128)(2,1)S(1)} %psum.7), channel_id=1, replica_groups=mesh['row'=4,'col'=8] {'row'}, dimensions={0}, use_global_device_ids=true | all-gather | bytes 81920 | tf_op jit(solution)/shard_map/all_gather | solution.py:75
  50.1 0.7 fusion.31
  50.8 0.7 compare_and_fusion
  51.5 0.6 gather_fusion.1
  52.0 1.2 %convolution_bitcast_fusion = f32[128,64]{1,0:T(8,128)S(1)} fusion(f32[4,128,64]{1,2,0:T(8,128)S(1)} %gather_fusion.1, bf16[1,4,64,64]{3,2,1,0:T(8,128)(2,1)} %param.18, f32[4]{0:T(128)S(1)} %get-tuple-element.6, pred[4]{0:T(512)(128)(4,1)S(1)} %get-tuple-element.5), kind=kOutput, calls=%fused_computation.9 | convolution fusion | flops 25231360 | bytes 196628 | tf_op jit(solution)/shard_map/fvk,fkl->vl/dot_general | solution.py:81
  53.3 0.0 collective-permute-done
  53.3 0.1 collective-permute-start.1
  53.3 0.0 collective-permute-done.7
  53.3 0.0 collective-permute-done.6
  53.4 5.0 %collective-permute-done.1 = bf16[1,1,128,384]{3,2,1,0:T(8,128)(2,1)S(1)} collective-permute-done((bf16[1,1,128,384]{3,2,1,0:T(8,128)(2,1)S(1)}, bf16[1,1,128,384]{3,2,1,0:T(8,128)(2,1)S(1)}, u32[]{:S(2)}, u32[]{:S(2)}) %collective-permute-start.1) | collective-permute-done | bytes 98336 | tf_op jit(solution)/shard_map/ppermute | solution.py:10
  58.4 0.0 collective-permute-start.2
  58.4 31.2 %all_gather.6 = bf16[3,8,128,64]{2,3,1,0:T(8,128)(2,1)S(1)} all-gather(bf16[3,1,128,64]{2,3,1,0:T(8,128)(2,1)S(1)} %pad_maximum_fusion.1), channel_id=1, replica_groups=mesh['row'=4,'col'=8] {'col'}, dimensions={1}, use_global_device_ids=true | all-gather | bytes 442368 | tf_op jit(solution)/shard_map/all_gather | solution.py:64
  89.6 0.0 collective-permute-start.3
  89.6 0.0 collective-permute-done.2
  89.6 2.2 %collective-permute-done.3 = bf16[1,1,128,384]{3,2,1,0:T(8,128)(2,1)S(1)} collective-permute-done((bf16[1,1,128,384]{3,2,1,0:T(8,128)(2,1)S(1)}, bf16[1,1,128,384]{3,2,1,0:T(8,128)(2,1)S(1)}, u32[]{:S(2)}, u32[]{:S(2)}) %collective-permute-start.3) | collective-permute-done | bytes 98336 | tf_op jit(solution)/shard_map/ppermute | solution.py:22
  91.8 3.0 %collective-permute-start.5 = (bf16[3,1,128,384]{3,2,1,0:T(8,128)(2,1)S(1)}, bf16[3,1,128,384]{3,2,1,0:T(8,128)(2,1)S(1)}, u32[]{:S(2)}, u32[]{:S(2)}) collective-permute-start(bf16[3,1,128,384]{3,2,1,0:T(8,128)(2,1)S(1)} %constant_dynamic-update-slice_fusion), channel_id=1, source_target_pairs={{1,0},{2,1},{3,2},{4,3},{5,4},{6,5},{7,6},{0,7},{9,8},{10,9},{11,1... | collective-permute-start | bytes 884744 | tf_op jit(solution)/shard_map/ppermute | solution.py:22
  94.8 0.0 collective-permute-start.4
  94.8 1.2 %convolution_bitcast_fusion.1 = f32[128,64]{1,0:T(8,128)S(1)} fusion(s32[]{:T(128)S(6)} %select_n.72, bf16[3,8,128,64]{2,3,1,0:T(8,128)(2,1)S(1)} %all_gather.6, bf16[1,1,3,5,64,64]{5,4,3,2,1,0:T(8,128)(2,1)} %param.17), kind=kOutput, calls=%fused_computation.10 | convolution fusion | flops 16515072 | bytes 548868 | tf_op jit(solution)/shard_map/dfvk,dfkl->vl/dot_general | solution.py:69
  96.0 0.0 copy-done.3
  96.1 0.8 convolution_add_fusion.1
  96.8 4.8 %collective-permute-done.5 = bf16[3,1,128,384]{3,2,1,0:T(8,128)(2,1)S(1)} collective-permute-done((bf16[3,1,128,384]{3,2,1,0:T(8,128)(2,1)S(1)}, bf16[3,1,128,384]{3,2,1,0:T(8,128)(2,1)S(1)}, u32[]{:S(2)}, u32[]{:S(2)}) %collective-permute-start.5) | collective-permute-done | bytes 294944 | tf_op jit(solution)/shard_map/ppermute | solution.py:22
  101.7 5.6 %collective-permute-done.4 = bf16[3,1,128,384]{3,2,1,0:T(8,128)(2,1)S(1)} collective-permute-done((bf16[3,1,128,384]{3,2,1,0:T(8,128)(2,1)S(1)}, bf16[3,1,128,384]{3,2,1,0:T(8,128)(2,1)S(1)}, u32[]{:S(2)}, u32[]{:S(2)}) %collective-permute-start.4) | collective-permute-done | bytes 294944 | tf_op jit(solution)/shard_map/ppermute | solution.py:20
  107.2 0.1 pad_maximum_fusion
  107.4 1.7 %gather_fusion = bf16[9,128,384]{2,1,0:T(8,128)(2,1)} fusion(bf16[9,128,384]{2,1,0:T(8,128)(2,1)S(1)} %bitcast.66, s32[1024]{0:T(1024)S(1)} %pad_clamp_fusion.1), kind=kCustom, calls=%fused_computation | custom fusion | bytes 1769508 | tf_op jit(solution)/shard_map/jit(_take)/gather | solution.py:47
  109.0 0.0 copy-start.1
  109.0 0.0 copy-start.2
  109.0 0.0 copy-done
  109.0 1.9 %fusion.2 = f32[128,384]{1,0:T(8,128)S(1)} fusion(bf16[1,1,9,384,384]{4,3,2,1,0:T(8,128)(2,1)S(1)} %copy-done, bf16[9,128,384]{2,1,0:T(8,128)(2,1)} %gather_fusion, pred[9]{0:T(512)(128)(4,1)S(1)} %get-tuple-element.9, pred[9]{0:T(512)(128)(4,1)S(1)} %get-tuple-element.10), kind=kOutput, calls=%fused_computation.5 | convolution fusion | flops 340623360 | bytes 3735570 | tf_op jit(solution)/shard_map/svp,spq->vq/dot_general | solution.py:51
  110.9 0.0 copy-done.1
  110.9 0.0 copy-done.2
  111.0 0.9 fusion.6
  (7 shorter events, 0.1 us)
Async XLA Ops:
  0.0 109.0 %copy-start = (bf16[1,1,9,384,384]{4,3,2,1,0:T(8,128)(2,1)S(1)}, bf16[1,1,9,384,384]{4,3,2,1,0:T(8,128)(2,1)}, u32[]{:S(2)}) copy-start(bf16[1,1,9,384,384]{4,3,2,1,0:T(8,128)(2,1)} %param.12) | copy-start | bytes 7962628
  0.0 96.0 %copy-start.3 = (bf16[1,1,64,64]{3,2,1,0:T(8,128)(2,1)S(1)}, bf16[1,1,64,64]{3,2,1,0:T(8,128)(2,1)}, u32[]{:S(2)}) copy-start(bf16[1,1,64,64]{3,2,1,0:T(8,128)(2,1)} %param.20) | copy-start | bytes 24580
  0.0 53.3 %collective-permute-start = (bf16[1,1,128,384]{3,2,1,0:T(8,128)(2,1)}, bf16[1,1,128,384]{3,2,1,0:T(8,128)(2,1)S(1)}, u32[]{:S(2)}, u32[]{:S(2)}) collective-permute-start(bf16[1,1,128,384]{3,2,1,0:T(8,128)(2,1)} %param.11), channel_id=1, source_target_pairs={{0,24},{8,0},{16,8},{24,16},{1,25},{9,1},{17,9},{25,17},{2,26},{10... | collective-permute-start | bytes 294920 | tf_op jit(solution)/shard_map/ppermute | solution.py:10
  3.5 49.8 %collective-permute-start.7 = (bf16[128,64]{0,1:T(8,128)(2,1)S(1)}, bf16[128,64]{0,1:T(8,128)(2,1)S(1)}, u32[]{:S(2)}, u32[]{:S(2)}) collective-permute-start(bf16[128,64]{0,1:T(8,128)(2,1)S(1)} %get-tuple-element.7), channel_id=1, source_target_pairs={{0,16},{8,24},{16,0},{24,8},{1,17},{9,25},{17,1},{25,9},{2,18},{10... | collective-permute-start | bytes 49160 | tf_op jit(solution)/shard_map/ppermute | solution.py:10
  4.3 49.1 %collective-permute-start.6 = (bf16[128,64]{0,1:T(8,128)(2,1)S(1)}, bf16[128,64]{0,1:T(8,128)(2,1)S(1)}, u32[]{:S(2)}, u32[]{:S(2)}) collective-permute-start(bf16[128,64]{0,1:T(8,128)(2,1)S(1)} %get-tuple-element.7), channel_id=1, source_target_pairs={{0,24},{8,0},{16,8},{24,16},{1,25},{9,1},{17,9},{25,17},{2,26},{10... | collective-permute-start | bytes 49160 | tf_op jit(solution)/shard_map/ppermute | solution.py:10
  53.3 5.1 %collective-permute-start.1 = (bf16[1,1,128,384]{3,2,1,0:T(8,128)(2,1)S(1)}, bf16[1,1,128,384]{3,2,1,0:T(8,128)(2,1)S(1)}, u32[]{:S(2)}, u32[]{:S(2)}) collective-permute-start(bf16[1,1,128,384]{3,2,1,0:T(8,128)(2,1)S(1)} %collective-permute-done), channel_id=1, source_target_pairs={{0,7},{1,0},{2,1},{3,2},{4,3},{5,4},{6,5},{7,6},{8,15},{9,8},{10,9... | collective-permute-start | bytes 294920 | tf_op jit(solution)/shard_map/ppermute | solution.py:10
  58.4 31.2 %collective-permute-start.2 = (bf16[1,1,128,384]{3,2,1,0:T(8,128)(2,1)S(1)}, bf16[1,1,128,384]{3,2,1,0:T(8,128)(2,1)S(1)}, u32[]{:S(2)}, u32[]{:S(2)}) collective-permute-start(bf16[1,1,128,384]{3,2,1,0:T(8,128)(2,1)S(1)} %collective-permute-done.1), channel_id=1, source_target_pairs={{0,8},{8,16},{16,24},{24,0},{1,9},{9,17},{17,25},{25,1},{2,10},{10... | collective-permute-start | bytes 294920 | tf_op jit(solution)/shard_map/ppermute | solution.py:20
  89.6 2.2 %collective-permute-start.3 = (bf16[1,1,128,384]{3,2,1,0:T(8,128)(2,1)S(1)}, bf16[1,1,128,384]{3,2,1,0:T(8,128)(2,1)S(1)}, u32[]{:S(2)}, u32[]{:S(2)}) collective-permute-start(bf16[1,1,128,384]{3,2,1,0:T(8,128)(2,1)S(1)} %collective-permute-done.1), channel_id=1, source_target_pairs={{8,0},{16,8},{24,16},{0,24},{9,1},{17,9},{25,17},{1,25},{10,2},{18... | collective-permute-start | bytes 294920 | tf_op jit(solution)/shard_map/ppermute | solution.py:22
  91.8 9.9 %collective-permute-start.5 = (bf16[3,1,128,384]{3,2,1,0:T(8,128)(2,1)S(1)}, bf16[3,1,128,384]{3,2,1,0:T(8,128)(2,1)S(1)}, u32[]{:S(2)}, u32[]{:S(2)}) collective-permute-start(bf16[3,1,128,384]{3,2,1,0:T(8,128)(2,1)S(1)} %constant_dynamic-update-slice_fusion), channel_id=1, source_target_pairs={{1,0},{2,1},{3,2},{4,3},{5,4},{6,5},{7,6},{0,7},{9,8},{10,9},{11,1... | collective-permute-start | bytes 884744 | tf_op jit(solution)/shard_map/ppermute | solution.py:22
  94.8 12.5 %collective-permute-start.4 = (bf16[3,1,128,384]{3,2,1,0:T(8,128)(2,1)S(1)}, bf16[3,1,128,384]{3,2,1,0:T(8,128)(2,1)S(1)}, u32[]{:S(2)}, u32[]{:S(2)}) collective-permute-start(bf16[3,1,128,384]{3,2,1,0:T(8,128)(2,1)S(1)} %constant_dynamic-update-slice_fusion), channel_id=1, source_target_pairs={{0,1},{1,2},{2,3},{3,4},{4,5},{5,6},{6,7},{7,0},{8,9},{9,10},{10,1... | collective-permute-start | bytes 884744 | tf_op jit(solution)/shard_map/ppermute | solution.py:20
  109.0 1.9 %copy-start.1 = (f32[128,64]{1,0:T(8,128)S(1)}, f32[128,64]{1,0:T(8,128)}, u32[]{:S(2)}) copy-start(f32[128,64]{1,0:T(8,128)} %convolution_add_fusion.1) | copy-start | bytes 98308
  109.0 1.9 %copy-start.2 = (bf16[1,1,64,384]{3,2,1,0:T(8,128)(2,1)S(1)}, bf16[1,1,64,384]{3,2,1,0:T(8,128)(2,1)}, u32[]{:S(2)}) copy-start(bf16[1,1,64,384]{3,2,1,0:T(8,128)(2,1)} %param.21) | copy-start | bytes 147460
where the time goes:
time: 112 us
  blocking collectives  74 us (66%)
  waiting for transfers between devices  17.6 us (16%)
  matrix products  7.99 us (7%)
  starting transfers between devices  6.36 us (6%)
  other arithmetic  2.8 us (2%)
  local copies, waits for them, and re-layouts  2.28 us (2%)
    psum x1, blocking collectives, per_device(): lax.psum(upward.astype(jnp.bfloat16), 'col').astype(jnp.float32)  37.6 us
    all_gather x1, blocking collectives, per_device(): lax.all_gather(three_rows[:, None].astype(jnp.bfloat16), 'col', axis=1, t...  31.2 us
    ppermute x2, waiting for transfers between devices, padded_2(): lax.ppermute(head, axis, [((i + 1) % count, i) for i in range(count)])  7.01 us
    ppermute x2, waiting for transfers between devices, padded_2(): lax.ppermute(tail, axis, [(i, (i + 1) % count) for i in range(count)])  5.56 us
    all_gather x1, blocking collectives, per_device(): lax.all_gather(own_region[None].astype(jnp.bfloat16), 'row', axis=0, tile...  5.22 us
    ppermute x4, waiting for transfers between devices, from_behind(): return lax.ppermute(value, axis, pairs)  5 us
    ppermute x4, starting transfers between devices, from_behind(): return lax.ppermute(value, axis, pairs)  3.37 us
    ppermute x2, starting transfers between devices, padded_2(): lax.ppermute(head, axis, [((i + 1) % count, i) for i in range(count)])  2.98 us
  transfers between devices with their start and end apart: 8, of which 4 were waited for; matrix products, arithmetic and copies ran while one was open for 8% of the time, Pallas kernels for 0%

commit v1 on v0

v1 whole, which is shorter than its diff:
```python
import functools

import jax
import jax.numpy as jnp
from jax import lax
from jax.experimental import pallas as pl
from jax.experimental.pallas import tpu as pltpu
from jax.sharding import PartitionSpec as P

REACH = 3
MESH = pl.DeviceIdType.MESH
BF16 = jnp.bfloat16
F32 = jnp.float32


def dot(a, b, dims):
    return lax.dot_general(a, b, (dims, ((), ())), preferred_element_type=F32)


def kernel(
    rows,
    cols,
    source_ref,
    count_ref,
    list_ref,
    vectors_hbm,
    blocks_hbm,
    basis_col_hbm,
    transfer_col_hbm,
    couple_hbm,
    coupling_hbm,
    transfer_row_hbm,
    basis_row_hbm,
    out_ref,
    table,
    blocks,
    basis_col,
    transfer_col,
    couple,
    coupling,
    transfer_row,
    basis_row,
    leaf_send,
    up_send,
    leaf_buf,
    region_buf,
    local_sems,
    near_send_sems,
    near_recv_sems,
    group_sems,
):
    r, c = lax.axis_index("row"), lax.axis_index("col")
    band = cols - REACH

    def behind(d, e):
        return (lax.rem(r + rows - d, rows), lax.rem(c + cols - e, cols))

    barrier = pltpu.get_barrier_semaphore()
    if rows * cols <= 64:
        for k in range(1, rows * cols):
            pl.semaphore_signal(barrier, inc=1, device_id=behind(k // cols, k % cols), device_id_type=MESH)
    else:

        @pl.loop(1, rows * cols)
        def _(k):
            pl.semaphore_signal(
                barrier, inc=1, device_id=behind(k // cols, lax.rem(k, cols)), device_id_type=MESH
            )

    loads = [
        pltpu.make_async_copy(src, dst, local_sems.at[i])
        for i, (src, dst) in enumerate(
            [
                (vectors_hbm, table.at[0]),
                (basis_col_hbm, basis_col),
                (transfer_col_hbm, transfer_col),
                (blocks_hbm, blocks),
                (couple_hbm, couple),
                (coupling_hbm, coupling),
                (transfer_row_hbm, transfer_row),
                (basis_row_hbm, basis_row),
            ]
        )
    ]
    for load in loads:
        load.start()
    for load in loads[:3]:
        load.wait()
    leaf = dot(basis_col[...], table[0], ((1,), (1,)))
    leaf_low = leaf.astype(BF16)
    leaf_send[...] = leaf_low
    up_send[...] = dot(transfer_col[...], leaf_low, ((0,), (0,))).astype(BF16)

    pl.semaphore_wait(barrier, rows * cols - 1)

    def send(src, dst, send_sem, recv_sem, target):
        copy = pltpu.make_async_remote_copy(
            src_ref=src, dst_ref=dst, send_sem=send_sem, recv_sem=recv_sem,
            device_id=target, device_id_type=MESH,
        )
        copy.start()
        return copy

    for d in range(REACH, rows):
        for e in range(cols):
            send(up_send, region_buf.at[(d - REACH) * cols + e], group_sems.at[0], group_sems.at[1], behind(d, e))
    near = {}
    for d, e in ((2, 2), (2, 1), (1, 2), (1, 1), (0, 2), (2, 0), (1, 0), (0, 1)):
        cell = d * REACH + e
        near[cell] = send(
            table.at[0], table.at[cell], near_send_sems.at[cell], near_recv_sems.at[cell], behind(d, e)
        )
    for d in range(REACH):
        for j in range(band):
            send(leaf_send, leaf_buf.at[d * band + j], group_sems.at[2], group_sems.at[3], behind(d, REACH + j))

    for load in loads[3:]:
        load.wait()

    count = count_ref[0, 0]

    def term(cell):
        slot = jnp.int32(0)
        for s in range(source_ref.shape[0]):
            slot = jnp.where(source_ref[s] == cell, s, slot)
        source = table[cell]
        source = jnp.where(slot < count, source, jnp.zeros_like(source))
        return dot(source, blocks[slot], ((1,), (0,)))

    total = term(0)
    for cell in (1, 3, 2, 6, 4, 5, 7, 8):
        near[cell].wait_recv()
        total = total + term(cell)

    pltpu.make_async_copy(region_buf, region_buf, group_sems.at[1]).wait()
    region_out = None
    for d in range(REACH, rows):
        target = lax.rem(r + d, rows)
        slot = jnp.int32(0)
        for f in range(rows):
            slot = jnp.where(list_ref[f] == target, f, slot)
        region = jnp.sum(region_buf[pl.ds((d - REACH) * cols, cols)].astype(F32), axis=0)
        part = dot(coupling[slot], region.astype(BF16), ((0,), (0,)))
        region_out = part if region_out is None else region_out + part
    leaf_out = dot(transfer_row[...], region_out.astype(BF16), ((0,), (0,)))
    pltpu.make_async_copy(leaf_buf, leaf_buf, group_sems.at[3]).wait()
    rank, vecs = leaf_buf.shape[1:]
    leaf_out = leaf_out + dot(
        couple[...].reshape(REACH * band * rank, rank),
        leaf_buf[...].reshape(REACH * band * rank, vecs),
        ((0,), (0,)),
    )
    total = total + dot(leaf_out.astype(BF16), basis_row[...], ((0,), (0,)))
    out_ref[...] = total.astype(out_ref.dtype)

    for copy in near.values():
        copy.wait_send()
    pltpu.make_async_copy(region_buf, region_buf, group_sems.at[0]).wait()
    pltpu.make_async_copy(leaf_buf, leaf_buf, group_sems.at[2]).wait()


def per_device(
    vectors,
    near_blocks,
    near_source,
    near_count,
    basis_col,
    transfer_col,
    leaf_couple,
    coupling,
    distant_region_list,
    transfer_row,
    basis_row,
):
    rows, cols = lax.axis_size("row"), lax.axis_size("col")
    vecs, leaf = vectors.shape[2:]
    rank = basis_col.shape[2]
    cells = near_blocks.shape[2]
    band = leaf_couple.shape[3]
    smem = pl.BlockSpec(memory_space=pltpu.SMEM)
    hbm = pl.BlockSpec(memory_space=pl.ANY)
    out = pl.pallas_call(
        functools.partial(kernel, rows, cols),
        out_shape=jax.ShapeDtypeStruct((vecs, leaf), BF16),
        in_specs=[smem] * 3 + [hbm] * 8,
        out_specs=pl.BlockSpec(memory_space=pltpu.VMEM),
        scratch_shapes=[
            pltpu.VMEM((cells, vecs, leaf), BF16),
            pltpu.VMEM((cells, leaf, leaf), BF16),
            pltpu.VMEM((rank, leaf), BF16),
            pltpu.VMEM((rank, rank), BF16),
            pltpu.VMEM((REACH * band, rank, rank), BF16),
            pltpu.VMEM((rows, rank, rank), BF16),
            pltpu.VMEM((rank, rank), BF16),
            pltpu.VMEM((rank, leaf), BF16),
            pltpu.VMEM((rank, vecs), BF16),
            pltpu.VMEM((rank, vecs), BF16),
            pltpu.VMEM((REACH * band, rank, vecs), BF16),
            pltpu.VMEM(((rows - REACH) * cols, rank, vecs), BF16),
            pltpu.SemaphoreType.DMA((8,)),
            pltpu.SemaphoreType.DMA((cells,)),
            pltpu.SemaphoreType.DMA((cells,)),
            pltpu.SemaphoreType.DMA((4,)),
        ],
        compiler_params=pltpu.CompilerParams(collective_id=0, has_side_effects=True),
    )(
        near_source[0, 0],
        near_count,
        distant_region_list[0],
        vectors[0, 0],
        near_blocks[0, 0],
        basis_col[0, 0],
        transfer_col[0, 0],
        leaf_couple[0, 0].reshape(REACH * band, rank, rank),
        coupling[0],
        transfer_row[0, 0],
        basis_row[0, 0],
    )
    return out[None, None]


def solution(mesh):
    placed = (
        P("row", "col", None, None),
        P("row", "col", None, None, None),
        P("row", "col", None),
        P("row", "col"),
        P("row", "col", None, None),
        P("row", "col", None, None),
        P("row", "col", None, None, None, None),
        P("row", None, None, None),
        P("row", None),
        P("row", "col", None, None),
        P("row", "col", None, None),
    )
    return jax.shard_map(
        per_device,
        mesh=mesh,
        in_specs=placed,
        out_specs=P("row", "col", None, None),
        check_vma=False,
    )
```

time: 112 us -> 35.3 us (0.32)
  blocking collectives: 74 us -> 0 us
  Pallas kernels: 0 us -> 33 us
  waiting for transfers between devices: 17.6 us -> 0 us
  matrix products: 7.99 us -> 0 us
  starting transfers between devices: 6.36 us -> 0 us
  other arithmetic: 2.8 us -> 0 us
    psum x1 -> x0, blocking collectives: 37.6 us -> none  [per_device(): lax.psum(upward.astype(jnp.bfloat16), 'col').astype(jnp.float32)]
    all_gather x2 -> x0, blocking collectives: 36.4 us -> none  [the longest x1 31.2 us: per_device(): lax.all_gather(three_rows[:, None].astype(jnp.bfloat16), 'col', axis=1, t...]
    pallas_call x0 -> x1, Pallas kernels: none -> 33 us  [per_device(): pl.pallas_call(functools.partial(kernel, rows, cols), out_shape=jax.Shape...]
    ppermute x8 -> x0, waiting for transfers between devices: 17.6 us -> none  [the longest x2 7.01 us: padded_2(): lax.ppermute(head, axis, [((i + 1) % count, i) for i in range(count)])]
    dot_general x7 -> x0, matrix products: 7.99 us -> none  [the longest x1 1.89 us: per_device(): jnp.einsum('svp,spq->vq', picked, near_blocks[0, 0], preferred_element_ty...]
    ppermute x8 -> x0, starting transfers between devices: 6.36 us -> none  [the longest x4 3.37 us: from_behind(): return lax.ppermute(value, axis, pairs)]
    gather x2 -> x0, local copies, waits for them, and re-layouts: 2.21 us -> none  [the longest x1 1.66 us: per_device(): picked = jnp.take(table, near_source[0, 0], axis=0)]
    unnamed x10 -> x1, local copies, waits for them, and re-layouts: 0.04 us -> 1.54 us
  transfers between devices with their start and end apart: 8 -> 0, of which waited for: 4 -> 0; matrix products, arithmetic and copies ran while one was open for 8% -> 0% of each run, Pallas kernels for 0% -> 0%
where the time goes in v1:
time: 35.3 us; the launch traced here: 35.2 us
  Pallas kernels  33 us (93%)
  local copies, waits for them, and re-layouts  1.54 us (4%)
  between operations  0.66 us (2%)
    pallas_call x1, Pallas kernels, per_device(): pl.pallas_call(functools.partial(kernel, rows, cols), out_shape=jax.Shape...  33 us
    unnamed x1, local copies, waits for them, and re-layouts  1.54 us

profile of v1, /device:TPU:0, one launch (start us, length us, event | category | flops | bytes accessed | tf_op | source)
XLA Modules:
  0.0 35.2 jit_solution(6216132173335763132)
XLA Ops:
  0.7 33.0 %shard_map.109 = bf16[128,384]{1,0:T(8,128)(2,1)} custom-call(s32[9]{0:T(128)} %bitcast.20, s32[1,1]{1,0:T(1,128)S(6)} %copy.13.count_ref, s32[4]{0:T(128)} %bitcast.21, bf16[128,384]{1,0:T(8,128)(2,1)} %bitcast.14, bf16[9,384,384]{2,1,0:T(8,128)(2,1)} %bitcast.11, bf16[64,384]{1,0:T(8,128)(2,1)} %bitcast.16, bf16[64,64]{1,0:T(8,128)(2,1)} %bitcast.18, ...), custom_call_target="tpu_custom_call" | custom-call | tf_op jit(solution)/shard_map/pallas_call | solution.py:182
  33.6 1.5 %copy.14 = bf16[1,1,128,384]{3,2,1,0:T(8,128)(2,1)} copy(bf16[1,1,128,384]{3,2,1,0:T(8,128)(2,1)} %bitcast.12) | data formatting | bytes 196608

commit v2 on v1

--- a/solution.py
+++ b/solution.py
@@ -42,7 +42,9 @@
     basis_row,
     leaf_send,
     up_send,
+    reduced_send,
     leaf_buf,
+    chunk_buf,
     region_buf,
     local_sems,
     near_send_sems,
@@ -86,34 +88,61 @@
         load.start()
     for load in loads[:3]:
         load.wait()
-    leaf = dot(basis_col[...], table[0], ((1,), (1,)))
-    leaf_low = leaf.astype(BF16)
+    leaf_low = dot(basis_col[...], table[0], ((1,), (1,))).astype(BF16)
     leaf_send[...] = leaf_low
-    up_send[...] = dot(transfer_col[...], leaf_low, ((0,), (0,))).astype(BF16)
+    up = dot(transfer_col[...], leaf_low, ((0,), (0,))).astype(BF16)
+    chunk = up_send.shape[1]
+    for e in range(cols):
+        up_send[e] = up[e * chunk : (e + 1) * chunk]
 
     pl.semaphore_wait(barrier, rows * cols - 1)
 
-    def send(src, dst, send_sem, recv_sem, target):
-        copy = pltpu.make_async_remote_copy(
+    def remote(src, dst, send_sem, recv_sem, target):
+        return pltpu.make_async_remote_copy(
             src_ref=src, dst_ref=dst, send_sem=send_sem, recv_sem=recv_sem,
             device_id=target, device_id_type=MESH,
         )
-        copy.start()
-        return copy
-
-    for d in range(REACH, rows):
-        for e in range(cols):
-            send(up_send, region_buf.at[(d - REACH) * cols + e], group_sems.at[0], group_sems.at[1], behind(d, e))
+
+    parity = lax.rem(r, 2)
+    partner = (r + 1 - 2 * parity, c)
+    odd, even = parity == 1, parity == 0
+
+    for e in range(1, cols):
+        remote(
+            up_send.at[lax.rem(c + cols - e, cols)], chunk_buf.at[e], group_sems.at[0], group_sems.at[1], behind(0, e)
+        ).start()
+    own_band = leaf_buf.at[pl.ds(0, band)]
+    mid_band = leaf_buf.at[pl.ds(band, band)]
+    top_band = leaf_buf.at[pl.ds(2 * band, band)]
+    for j in range(band):
+        remote(leaf_send, leaf_buf.at[j], group_sems.at[2], group_sems.at[3], behind(0, REACH + j)).start()
     near = {}
-    for d, e in ((2, 2), (2, 1), (1, 2), (1, 1), (0, 2), (2, 0), (1, 0), (0, 1)):
+    for d, e in ((2, 0), (0, 2), (0, 1), (2, 1), (2, 2)):
         cell = d * REACH + e
-        near[cell] = send(
+        near[cell] = remote(
             table.at[0], table.at[cell], near_send_sems.at[cell], near_recv_sems.at[cell], behind(d, e)
         )
-    for d in range(REACH):
-        for j in range(band):
-            send(leaf_send, leaf_buf.at[d * band + j], group_sems.at[2], group_sems.at[3], behind(d, REACH + j))
-
+        near[cell].start()
+    for e in range(REACH):
+        cell = REACH + e
+        near[cell] = remote(
+            table.at[2 * REACH * (1 - parity) + e],
+            table.at[cell],
+            near_send_sems.at[cell],
+            near_recv_sems.at[cell],
+            partner,
+        )
+    band_up = remote(own_band, top_band, group_sems.at[4], group_sems.at[5], behind(2, 0))
+    band_across = remote(
+        leaf_buf.at[pl.ds(2 * band * (1 - parity), band)], mid_band, group_sems.at[6], group_sems.at[7], partner
+    )
+
+    def start_if(condition, copy):
+        @pl.when(condition)
+        def _():
+            copy.start()
+
+    start_if(odd, near[REACH])
     for load in loads[3:]:
         load.wait()
 
@@ -127,36 +156,70 @@
         source = jnp.where(slot < count, source, jnp.zeros_like(source))
         return dot(source, blocks[slot], ((1,), (0,)))
 
+    arrived = chunk_buf.at[pl.ds(1, cols - 1)]
+    pltpu.make_async_copy(arrived, arrived, group_sems.at[1]).wait()
+    reduced = up_send[c].astype(F32)
+    for e in range(1, cols):
+        reduced = reduced + chunk_buf[e].astype(F32)
+    reduced_send[...] = reduced.astype(BF16)
+    pltpu.make_async_copy(own_band, own_band, group_sems.at[3]).wait()
+    band_up.start()
+    start_if(odd, band_across)
     total = term(0)
-    for cell in (1, 3, 2, 6, 4, 5, 7, 8):
-        near[cell].wait_recv()
-        total = total + term(cell)
-
-    pltpu.make_async_copy(region_buf, region_buf, group_sems.at[1]).wait()
+    for d in range(REACH, rows):
+        for e in range(cols):
+            remote(
+                reduced_send, region_buf.at[d - REACH, c], group_sems.at[8], group_sems.at[9], behind(d, e)
+            ).start()
+
+    near[2 * REACH].wait_recv()
+    start_if(even, near[REACH])
+    total = total + term(2 * REACH)
+    band_up.wait_recv()
+    start_if(even, band_across)
+    for e in (2, 1):
+        near[e].wait_recv()
+        start_if(odd, near[REACH + e])
+        total = total + term(e)
+    near[REACH].wait_recv()
+    total = total + term(REACH)
+
+    pltpu.make_async_copy(region_buf, region_buf, group_sems.at[9]).wait()
+    rank, vecs = leaf_buf.shape[1:]
     region_out = None
     for d in range(REACH, rows):
         target = lax.rem(r + d, rows)
         slot = jnp.int32(0)
         for f in range(rows):
             slot = jnp.where(list_ref[f] == target, f, slot)
-        region = jnp.sum(region_buf[pl.ds((d - REACH) * cols, cols)].astype(F32), axis=0)
-        part = dot(coupling[slot], region.astype(BF16), ((0,), (0,)))
+        region = region_buf[d - REACH].astype(F32).reshape(rank, vecs).astype(BF16)
+        part = dot(coupling[slot], region, ((0,), (0,)))
         region_out = part if region_out is None else region_out + part
     leaf_out = dot(transfer_row[...], region_out.astype(BF16), ((0,), (0,)))
-    pltpu.make_async_copy(leaf_buf, leaf_buf, group_sems.at[3]).wait()
-    rank, vecs = leaf_buf.shape[1:]
+    band_across.wait_recv()
     leaf_out = leaf_out + dot(
         couple[...].reshape(REACH * band * rank, rank),
         leaf_buf[...].reshape(REACH * band * rank, vecs),
         ((0,), (0,)),
     )
     total = total + dot(leaf_out.astype(BF16), basis_row[...], ((0,), (0,)))
+
+    for e in (1, 2):
+        near[2 * REACH + e].wait_recv()
+        start_if(even, near[REACH + e])
+        total = total + term(2 * REACH + e)
+    for e in (1, 2):
+        near[REACH + e].wait_recv()
+        total = total + term(REACH + e)
     out_ref[...] = total.astype(out_ref.dtype)
 
     for copy in near.values():
         copy.wait_send()
-    pltpu.make_async_copy(region_buf, region_buf, group_sems.at[0]).wait()
-    pltpu.make_async_copy(leaf_buf, leaf_buf, group_sems.at[2]).wait()
+    band_up.wait_send()
+    band_across.wait_send()
+    pltpu.make_async_copy(arrived, arrived, group_sems.at[0]).wait()
+    pltpu.make_async_copy(own_band, own_band, group_sems.at[2]).wait()
+    pltpu.make_async_copy(region_buf, region_buf, group_sems.at[8]).wait()
 
 
 def per_device(
@@ -194,13 +257,15 @@
             pltpu.VMEM((rank, rank), BF16),
             pltpu.VMEM((rank, leaf), BF16),
             pltpu.VMEM((rank, vecs), BF16),
-            pltpu.VMEM((rank, vecs), BF16),
+            pltpu.VMEM((cols, rank // cols, vecs), BF16),
+            pltpu.VMEM((rank // cols, vecs), BF16),
             pltpu.VMEM((REACH * band, rank, vecs), BF16),
-            pltpu.VMEM(((rows - REACH) * cols, rank, vecs), BF16),
+            pltpu.VMEM((cols, rank // cols, vecs), BF16),
+            pltpu.VMEM((rows - REACH, cols, rank // cols, vecs), BF16),
             pltpu.SemaphoreType.DMA((8,)),
             pltpu.SemaphoreType.DMA((cells,)),
             pltpu.SemaphoreType.DMA((cells,)),
-            pltpu.SemaphoreType.DMA((4,)),
+            pltpu.SemaphoreType.DMA((10,)),
         ],
         compiler_params=pltpu.CompilerParams(collective_id=0, has_side_effects=True),
     )(

time: 35.3 us -> 25.6 us (0.73)
  Pallas kernels: 33 us -> 23.1 us
    pallas_call x1, Pallas kernels: 33 us -> 23.1 us  [per_device(): pl.pallas_call(functools.partial(kernel, rows, cols), out_shape=jax.Shape...]
where the time goes in v2:
time: 25.6 us; the launch traced here: 25.3 us
  Pallas kernels  23.1 us (90%)
  local copies, waits for them, and re-layouts  1.54 us (6%)
  between operations  0.66 us (3%)
    pallas_call x1, Pallas kernels, per_device(): pl.pallas_call(functools.partial(kernel, rows, cols), out_shape=jax.Shape...  23.1 us
    unnamed x1, local copies, waits for them, and re-layouts  1.54 us

profile of v2, /device:TPU:0, one launch (start us, length us, event | category | flops | bytes accessed | tf_op | source)
XLA Modules:
  0.0 25.3 jit_solution(9107940906880863990)
XLA Ops:
  0.7 23.1 %shard_map.109 = bf16[128,384]{1,0:T(8,128)(2,1)} custom-call(s32[9]{0:T(128)} %bitcast.20, s32[1,1]{1,0:T(1,128)S(6)} %copy.13.count_ref, s32[4]{0:T(128)} %bitcast.21, bf16[128,384]{1,0:T(8,128)(2,1)} %bitcast.14, bf16[9,384,384]{2,1,0:T(8,128)(2,1)} %bitcast.11, bf16[64,384]{1,0:T(8,128)(2,1)} %bitcast.16, bf16[64,64]{1,0:T(8,128)(2,1)} %bitcast.18, ...), custom_call_target="tpu_custom_call" | custom-call | tf_op jit(solution)/shard_map/pallas_call | solution.py:245
  23.8 1.5 %copy.14 = bf16[1,1,128,384]{3,2,1,0:T(8,128)(2,1)} copy(bf16[1,1,128,384]{3,2,1,0:T(8,128)(2,1)} %bitcast.12) | data formatting | bytes 196608
